TPU v7x, 8 devices: a whole 2x2x1 slice. The times are simulated.
8 devices in a mesh: rep: 2 (over y, z), dp: 4 (over x, core).
Axes of the slice: x: 2, y: 2, z: 1, core: 2. Of those that a mesh axis runs over, the one named last changes fastest.
Arguments:
- a: bfloat16 [8, 4, 4096, 896], P(('rep', 'dp')), parts along dimension 0
- g: bfloat16 [8, 4, 4096, 2304], P(('rep', 'dp')), parts along dimension 0
Outputs:
- output: bfloat16 [8, 896, 2304], P('rep'), parts along dimension 0
There are 2 independent parts. A program takes and returns all parts, laid end to end along the dimension named above; each array names one.
All inputs are finite; a program needn't handle non-finite values.
Results may differ from a plain program's by a relative error of at most 0.012.
Values are sent between devices in bfloat16 or wider.
A program may use at most 2 GiB of HBM per device.

v0:
```python
import jax
import jax.numpy as jnp


def solution(mesh):
    groups = mesh.shape["rep"]

    def step(a, g):
        a, g = (t.reshape(groups, -1, *t.shape[1:]) for t in (a, g))
        sums = jnp.einsum("rsntd,rsntf->rndf", a, g, preferred_element_type=jnp.float32)
        return sums.astype(jnp.bfloat16).reshape(-1, *sums.shape[2:])

    return step
```

profile of v0, /device:TPU:0, one launch (start us, length us, event | category | flops | bytes accessed | tf_op | source)
XLA Modules:
  0.0 641.1 jit_solution(2141290238833178782)
XLA Ops:
  0.0 78.6 %fusion.3 = f32[1,4,896,2304]{3,2,1,0:T(8,128)} fusion(bf16[1,4,4096,2304]{3,2,1,0:T(8,128)(2,1)} %param.1, bf16[1,4,4096,896]{3,2,1,0:T(8,128)(2,1)} %param), kind=kOutput, calls=%fused_computation.3 | convolution fusion | flops 67645734912 | bytes 137887744 | tf_op jit(solution)/rsntd,rsntf->rndf/dot_general | solution.py:10
  78.6 562.4 %all-reduce.2 = bf16[1,4,896,2304]{3,2,1,0:T(8,128)(2,1)} all-reduce(f32[1,4,896,2304]{3,2,1,0:T(8,128)} %fusion.3), channel_id=1, replica_groups=[2,4]<=[8], use_global_device_ids=true, to_apply=%add.clone | all-reduce | flops 8257536 | bytes 49545216 | tf_op jit(solution)/rsntd,rsntf->rndf/dot_general | solution.py:10
where the time goes:
time: 641 us
  blocking collectives  562 us (88%)
  matrix products  78.6 us (12%)
    dot_general x1, blocking collectives, step(): jnp.einsum('rsntd,rsntf->rndf', a, g, preferred_element_type=jnp.float32)  562 us
    dot_general x1, matrix products, step(): jnp.einsum('rsntd,rsntf->rndf', a, g, preferred_element_type=jnp.float32)  78.6 us

commit v1 on v0

v1 whole, which is shorter than its diff:
```python
import jax
import jax.numpy as jnp
from jax import lax
from jax.experimental import pallas as pl
from jax.experimental.pallas import tpu as pltpu
from jax.sharding import PartitionSpec as P

MESH = pl.DeviceIdType.MESH
COLS = 256
STRIP = 128
G_SLOTS = 3
LAG = 2


def kernel(
    a_ref, g_ref, out_ref,
    at, raw, gs, p_send, acc, s_own, s_recv,
    a_sem, g_sem, ps_sem, p0_sem, pr_sem, xs_sem, xr_sem, rs_sem, rr_sem,
):
    n_mat, rows, cols = out_ref.shape
    half = rows // 2
    per = cols // COLS
    panels = n_mat * per
    strips = rows // STRIP

    me = lax.axis_index("dp")
    core = lax.rem(me, 2)
    sibling = me + 1 - 2 * core
    peer = lax.rem(me + 2, 4)
    own = pl.multiple_of(core * half, half)
    other = pl.multiple_of((1 - core) * half, half)

    def load_strip(n, r, slot):
        c = pl.multiple_of(r * STRIP, STRIP)
        return pltpu.make_async_copy(a_ref.at[0, n, :, pl.ds(c, STRIP)], raw.at[slot], a_sem.at[slot])

    def load_panel(p):
        c = pl.multiple_of(lax.rem(p, per) * COLS, COLS)
        slot = lax.rem(p, G_SLOTS)
        return pltpu.make_async_copy(g_ref.at[0, p // per, :, pl.ds(c, COLS)], gs.at[slot], g_sem.at[slot])

    def tile(p, first, size):
        c = pl.multiple_of(lax.rem(p, per) * COLS, COLS)
        return out_ref.at[p // per, pl.ds(first, size), pl.ds(c, COLS)]

    def send_partial(p, lo, size, recv):
        slot = lax.rem(p, 2)
        return pltpu.make_async_remote_copy(
            src_ref=p_send.at[slot, pl.ds(lo, size)], dst_ref=tile(p, other + lo, size),
            send_sem=ps_sem.at[slot], recv_sem=recv,
            device_id={"dp": sibling}, device_id_type=MESH)

    def recv_partial(p, lo, size, recv):
        return pltpu.make_async_remote_copy(
            src_ref=p_send.at[0, pl.ds(lo, size)], dst_ref=tile(p, own + lo, size),
            send_sem=ps_sem.at[0], recv_sem=recv,
            device_id={"dp": sibling}, device_id_type=MESH)

    def exchange(p, lo, size):
        return pltpu.make_async_remote_copy(
            src_ref=s_own.at[p, pl.ds(lo, size)], dst_ref=s_recv.at[p, pl.ds(lo, size)],
            send_sem=xs_sem, recv_sem=xr_sem.at[p],
            device_id={"dp": peer}, device_id_type=MESH)

    def forward(p):
        return pltpu.make_async_remote_copy(
            src_ref=tile(p, own, half), dst_ref=tile(p, own, half),
            send_sem=rs_sem, recv_sem=rr_sem,
            device_id={"dp": sibling}, device_id_type=MESH)

    def dot(first, size, slot):
        return lax.dot_general(
            at[pl.ds(first, size)], gs[slot], (((1,), (0,)), ((), ())), preferred_element_type=jnp.float32)

    def chip_sum(p, lo, size):
        got = tile(p, own + lo, size)[...].astype(jnp.float32)
        s_own[p, pl.ds(lo, size)] = (acc[pl.ds(lo, size)] + got).astype(s_own.dtype)

    def combine(p):
        exchange(p, 0, half).wait_recv()
        both = s_own[p].astype(jnp.float32) + s_recv[p].astype(jnp.float32)
        tile(p, own, half)[...] = both.astype(out_ref.dtype)
        forward(p).start()

    def flip(r):
        load_strip(0, r, r).wait()
        at[pl.ds(pl.multiple_of(r * STRIP, STRIP), STRIP)] = raw[r].T

    order = []
    for i in range(strips // 2):
        order += [(1 - core) * (strips // 2 + 1) + i, core * (strips // 2 + 1) + i]
    load_strip(0, order[0], order[0]).start()
    load_panel(0).start()
    load_strip(0, order[1], order[1]).start()
    for r in order[2:] + [strips // 2]:
        load_strip(0, r, r).start()
    for p in range(1, G_SLOTS):
        load_panel(p).start()

    barrier = pltpu.get_barrier_semaphore()
    for d in (sibling, peer):
        pl.semaphore_signal(barrier, inc=1, device_id={"dp": d}, device_id_type=MESH)
    pl.semaphore_wait(barrier, 2)

    blocks = [(i * STRIP, STRIP) for i in range(strips // 2)] + [(strips // 2 * STRIP, STRIP // 2)]

    def place(h, i):
        lo, size = blocks[i]
        if i == len(blocks) - 1:
            lo = (1 - h) * lo
        else:
            lo = lo + h * (STRIP // 2)
        return pl.multiple_of(h * half + lo, STRIP // 2), pl.multiple_of(lo, STRIP // 2), size

    def first(i):
        if i < len(blocks) - 1:
            flip(order[2 * i])
        else:
            flip(strips // 2)
        row, lo, size = place(1 - core, i)
        if i == 0:
            load_panel(0).wait()
        p_send[0, pl.ds(lo, size)] = dot(row, size, 0).astype(p_send.dtype)
        send_partial(0, lo, size, p0_sem.at[i]).start()

    def second(i):
        if i < len(blocks) - 1:
            flip(order[2 * i + 1])
        row, lo, size = place(core, i)
        acc[pl.ds(lo, size)] = dot(row, size, 0)

    def third(i):
        _, lo, size = place(core, i)
        recv_partial(0, lo, size, p0_sem.at[i]).wait_recv()
        chip_sum(0, lo, size)
        exchange(0, lo, size).start()

    first(0)
    for i in range(len(blocks)):
        second(i)
        if i + 1 < len(blocks):
            first(i + 1)
        third(i)
    load_panel(G_SLOTS).start()

    def step(p, carry):
        n, j = p // per, lax.rem(p, per)
        slot, ps = lax.rem(p, G_SLOTS), lax.rem(p, 2)

        @pl.when(j == 0)
        def _():
            def turn(r, c):
                flip(r)
                return c

            lax.fori_loop(0, strips, turn, 0)

        @pl.when((j == 1) & (n < n_mat - 1))
        def _():
            def more(r, c):
                load_strip(n + 1, r, r).start()
                return c

            lax.fori_loop(0, strips, more, 0)

        load_panel(p).wait()

        @pl.when(p >= 2)
        def _():
            send_partial(p - 2, 0, half, pr_sem.at[p - 2]).wait_send()

        p_send[ps] = dot(other, half, slot).astype(p_send.dtype)

        @pl.when(p >= 2)
        def _():
            recv_partial(p - 1, 0, half, pr_sem.at[p - 1]).wait_recv()
            chip_sum(p - 1, 0, half)

        send_partial(p, 0, half, pr_sem.at[p]).start()
        acc[...] = dot(own, half, slot)

        @pl.when(p >= 2)
        def _():
            exchange(p - 1, 0, half).start()

        @pl.when(p + G_SLOTS < panels)
        def _():
            load_panel(p + G_SLOTS).start()

        @pl.when(p >= LAG + 1)
        def _():
            combine(p - 1 - LAG)

        return carry

    lax.fori_loop(1, panels, step, 0)

    last = panels - 1
    recv_partial(last, 0, half, pr_sem.at[last]).wait_recv()
    chip_sum(last, 0, half)
    exchange(last, 0, half).start()

    def drain(p, carry):
        combine(p)
        return carry

    lax.fori_loop(last - LAG, panels, drain, 0)

    for p in (last - 1, last):
        send_partial(p, 0, half, pr_sem.at[p]).wait_send()

    def everything(send, recv):
        return pltpu.make_async_remote_copy(
            src_ref=s_own, dst_ref=s_recv, send_sem=send, recv_sem=recv,
            device_id={"dp": sibling}, device_id_type=MESH)

    everything(xs_sem, rr_sem).wait_send()
    everything(rs_sem, rr_sem).wait()


def solution(mesh):
    def sums(a, g):
        _, n, tokens, d = a.shape
        ff = g.shape[-1]
        half, panels, strips = d // 2, n * ff // COLS, d // STRIP
        dma = pltpu.SemaphoreType.DMA
        return pl.pallas_call(
            kernel,
            out_shape=pltpu.VMEM((n, d, ff), jnp.bfloat16),
            in_specs=[pl.BlockSpec(memory_space=pl.ANY)] * 2,
            out_specs=pl.BlockSpec(memory_space=pltpu.VMEM),
            scratch_shapes=[
                pltpu.VMEM((d, tokens), jnp.bfloat16),
                pltpu.VMEM((strips, tokens, STRIP), jnp.bfloat16),
                pltpu.VMEM((G_SLOTS, tokens, COLS), jnp.bfloat16),
                pltpu.VMEM((2, half, COLS), jnp.bfloat16),
                pltpu.VMEM((half, COLS), jnp.float32),
                pltpu.VMEM((panels, half, COLS), jnp.bfloat16),
                pltpu.VMEM((panels, half, COLS), jnp.bfloat16),
                dma((strips,)), dma((G_SLOTS,)), dma((2,)), dma((4,)), dma((panels,)),
                dma, dma((panels,)), dma, dma,
            ],
            compiler_params=pltpu.CompilerParams(
                collective_id=0, has_side_effects=True, vmem_limit_bytes=46 * 1024 * 1024
            ),
            name="sums",
        )(a, g)

    return jax.shard_map(
        sums, mesh=mesh, in_specs=(P(("rep", "dp")),) * 2, out_specs=P("rep"), check_vma=False
    )
```

time: 641 us -> 203 us (0.32)
  blocking collectives: 562 us -> 0 us
  Pallas kernels: 0 us -> 197 us
  matrix products: 78.6 us -> 0 us
    dot_general x1 -> x0, blocking collectives: 562 us -> none  [step(): jnp.einsum('rsntd,rsntf->rndf', a, g, preferred_element_type=jnp.float32)]
    pallas_call x0 -> x1, Pallas kernels: none -> 197 us  [sums(): pl.pallas_call(kernel, out_shape=pltpu.VMEM((n, d, ff), jnp.bfloat16), in...]
    dot_general x1 -> x0, matrix products: 78.6 us -> none  [step(): jnp.einsum('rsntd,rsntf->rndf', a, g, preferred_element_type=jnp.float32)]
where the time goes in v1:
time: 203 us
  Pallas kernels  197 us (97%)
  local copies, waits for them, and re-layouts  6.07 us (3%)
    pallas_call x1, Pallas kernels, sums(): pl.pallas_call(kernel, out_shape=pltpu.VMEM((n, d, ff), jnp.bfloat16), in...  197 us
    unnamed x1, local copies, waits for them, and re-layouts  6.07 us

profile of v1, /device:TPU:0, one launch (start us, length us, event | category | flops | bytes accessed | tf_op | source)
XLA Modules:
  0.0 203.4 jit_solution(3718764202266071420)
XLA Ops:
  0.0 197.3 %sums.1 = bf16[4,896,2304]{2,1,0:T(8,128)(2,1)S(1)} custom-call(bf16[1,4,4096,896]{3,2,1,0:T(8,128)(2,1)} %a_ref.1, bf16[1,4,4096,2304]{3,2,1,0:T(8,128)(2,1)} %g_ref.1), custom_call_target="tpu_custom_call" | custom-call | tf_op jit(solution)/shard_map/sums/pallas_call | solution.py:227
  197.3 6.1 %copy.4 = bf16[4,896,2304]{2,1,0:T(8,128)(2,1)} copy(bf16[4,896,2304]{2,1,0:T(8,128)(2,1)S(1)} %sums.1) | data formatting | bytes 33030144

commit v2 on v0

v2 whole, which is shorter than its diff:
```python
import jax
import jax.numpy as jnp
from jax import lax
from jax.experimental import pallas as pl
from jax.experimental.pallas import tpu as pltpu
from jax.sharding import PartitionSpec as P

MESH = pl.DeviceIdType.MESH
COLS = 256
STRIP = 128
G_SLOTS = 3
LAG = 4


def kernel(
    a_ref, g_ref, out_ref,
    at, raw, gs, p_send, acc, s_own, s_recv,
    a_sem, g_sem, ps_sem, p0_sem, pr_sem, xs_sem, xr_sem, rs_sem, rr_sem,
):
    n_mat, rows, cols = out_ref.shape
    half = rows // 2
    size = half // 2
    per = cols // COLS
    panels = n_mat * per
    strips = rows // STRIP
    pairs = strips // 2
    rest = STRIP // 2

    me = lax.axis_index("dp")
    core = lax.rem(me, 2)
    sibling = me + 1 - 2 * core
    peer = lax.rem(me + 2, 4)
    own = pl.multiple_of(core * half, half)
    other = pl.multiple_of((1 - core) * half, half)

    def load_strip(n, r, slot):
        c = pl.multiple_of(r * STRIP, STRIP)
        return pltpu.make_async_copy(a_ref.at[0, n, :, pl.ds(c, STRIP)], raw.at[slot], a_sem.at[slot])

    def load_panel(p):
        c = pl.multiple_of(lax.rem(p, per) * COLS, COLS)
        slot = lax.rem(p, G_SLOTS)
        return pltpu.make_async_copy(g_ref.at[0, p // per, :, pl.ds(c, COLS)], gs.at[slot], g_sem.at[slot])

    def tile(p, first, n):
        c = pl.multiple_of(lax.rem(p, per) * COLS, COLS)
        return out_ref.at[p // per, pl.ds(first, n), pl.ds(c, COLS)]

    def remote(src, dst, send, recv, to):
        return pltpu.make_async_remote_copy(
            src_ref=src, dst_ref=dst, send_sem=send, recv_sem=recv,
            device_id={"dp": to}, device_id_type=MESH)

    def exchange(p, lo, n, recv):
        return remote(s_own.at[p, pl.ds(lo, n)], s_recv.at[p, pl.ds(lo, n)], xs_sem, recv, peer)

    def chip_sum(p, lo, n, mine):
        got = tile(p, own + lo, n)[...].astype(jnp.float32)
        s_own[p, pl.ds(lo, n)] = (mine[...] + got).astype(s_own.dtype)

    def flip(r):
        load_strip(0, r, r).wait()
        at[pl.ds(pl.multiple_of(r * STRIP, STRIP), STRIP)] = raw[r].T

    def dot(first, n, slot):
        return lax.dot_general(
            at[pl.ds(first, n)], gs[slot], (((1,), (0,)), ((), ())), preferred_element_type=jnp.float32)

    def strip(k):
        h = core + (1 - 2 * core) * (1 - lax.rem(k, 2))
        mid = k // (2 * pairs)
        return (1 - mid) * (h * (pairs + 1) + k // 2) + mid * pairs, h

    def lower(h, i):
        return pl.multiple_of(h * rest + i * STRIP, rest)

    load_strip(0, *[strip(0)[0]] * 2).start()
    load_panel(0).start()

    def load(k, c):
        load_strip(0, *[strip(k)[0]] * 2).start()
        return c

    lax.fori_loop(1, strips, load, 0)
    for p in range(1, G_SLOTS):
        load_panel(p).start()

    barrier = pltpu.get_barrier_semaphore()
    for d in (sibling, peer):
        pl.semaphore_signal(barrier, inc=1, device_id={"dp": d}, device_id_type=MESH)

    def send_strip(lo, n, i):
        return remote(p_send.at[0, pl.ds(lo, n)], tile(0, other + lo, n), ps_sem.at[0], p0_sem.at[i], sibling)

    def take_strip(lo, n, i):
        remote(p_send.at[0, pl.ds(lo, n)], tile(0, own + lo, n), ps_sem.at[0], p0_sem.at[i], sibling).wait_recv()
        chip_sum(0, lo, n, acc.at[pl.ds(lo, n)])
        exchange(0, lo, n, xr_sem.at[0]).start()

    flat = acc.at[pl.ds(half, STRIP)]

    def fill(k, carry):
        r, h = strip(k)
        i = k // 2
        flip(r)

        @pl.when(k == 0)
        def _():
            load_panel(0).wait()

        flat[...] = dot(pl.multiple_of(r * STRIP, STRIP), STRIP, 0)

        @pl.when((lax.rem(k, 2) == 0) & (k < 2 * pairs))
        def _():
            lo = lower(h, i)
            p_send[0, pl.ds(lo, STRIP)] = flat[...].astype(p_send.dtype)

            @pl.when(k == 0)
            def _():
                pl.semaphore_wait(barrier, 2)

            send_strip(lo, STRIP, i).start()

        @pl.when(lax.rem(k, 2) == 1)
        def _():
            acc[pl.ds(lower(h, i), STRIP)] = flat[...]

        @pl.when(k == 2 * pairs)
        def _():
            lo = pl.multiple_of(core * pairs * STRIP, rest)
            theirs = pl.multiple_of((1 - core) * rest, rest)
            p_send[0, pl.ds(lo, rest)] = flat[pl.ds(theirs, rest)].astype(p_send.dtype)
            send_strip(lo, rest, pairs).start()
            mine = pl.multiple_of(core * rest, rest)
            acc[pl.ds(pl.multiple_of((1 - core) * pairs * STRIP, rest), rest)] = flat[pl.ds(mine, rest)]

        @pl.when((lax.rem(k, 2) == 0) & (k >= 2))
        def _():
            take_strip(lower(core, i - 1), STRIP, i - 1)

        return carry

    lax.fori_loop(0, strips, fill, 0)
    take_strip(pl.multiple_of((1 - core) * pairs * STRIP, rest), rest, pairs)
    load_panel(G_SLOTS).start()

    def spot(k):
        return k // 2, pl.multiple_of(lax.rem(k, 2) * size, size)

    def send_partial(k):
        p, lo = spot(k)
        slot = lax.rem(k, 2)
        return remote(p_send.at[slot, pl.ds(0, size)], tile(p, other + lo, size), ps_sem.at[slot], pr_sem.at[k], sibling)

    def finish(k):
        p, lo = spot(k)
        remote(p_send.at[0, pl.ds(0, size)], tile(p, own + lo, size), ps_sem.at[0], pr_sem.at[k], sibling).wait_recv()
        chip_sum(p, lo, size, acc.at[pl.ds(size, size)])

    def leave(k):
        p, lo = spot(k)
        return exchange(p, lo, size, xr_sem.at[k])

    def combine(k):
        @pl.when(k == 1)
        def _():
            exchange(0, 0, half, xr_sem.at[0]).wait_recv()

        @pl.when(k > 1)
        def _():
            leave(k).wait_recv()

        def one(k, c):
            p, lo = spot(k)
            both = s_own[p, pl.ds(lo, size)].astype(jnp.float32) + s_recv[p, pl.ds(lo, size)].astype(jnp.float32)
            here = tile(p, own + lo, size)
            here[...] = both.astype(out_ref.dtype)
            remote(here, here, rs_sem, rr_sem, sibling).start()
            return c

        lax.fori_loop(k - 1 // k, k + 1, one, 0)

    def step(q, carry):
        k, t = q // 2, lax.rem(q, 2)
        p, b = k // 2, lax.rem(k, 2)
        n, j = p // per, lax.rem(p, per)

        @pl.when((b == 0) & (t == 0))
        def _():
            load_panel(p).wait()

            @pl.when(j == 0)
            def _():
                def turn(r, c):
                    flip(r)
                    return c

                lax.fori_loop(0, strips, turn, 0)

            @pl.when((j == 1) & (n < n_mat - 1))
            def _():
                def more(r, c):
                    load_strip(n + 1, r, r).start()
                    return c

                lax.fori_loop(0, strips, more, 0)

        h = core + (1 - 2 * core) * (1 - t)
        acc[pl.ds(pl.multiple_of(t * size, size), size)] = dot(
            pl.multiple_of((2 * h + b) * size, size), size, lax.rem(p, G_SLOTS))

        @pl.when(t == 0)
        def _():
            @pl.when(k == 2)
            def _():
                send_strip(0, half, 0).wait_send()

            @pl.when(k >= 4)
            def _():
                send_partial(k - 2).wait_send()

            p_send[lax.rem(k, 2), pl.ds(0, size)] = acc[pl.ds(0, size)].astype(p_send.dtype)

        @pl.when((t == 0) & (k >= 3))
        def _():
            finish(k - 1)

        @pl.when(t == 0)
        def _():
            send_partial(k).start()

        @pl.when((t == 0) & (k >= 3))
        def _():
            leave(k - 1).start()

        @pl.when((t == 1) & (b == 1) & (p + G_SLOTS < panels))
        def _():
            load_panel(p + G_SLOTS).start()

        @pl.when((t == 1) & (k - 1 - LAG >= 1))
        def _():
            combine(k - 1 - LAG)

        return carry

    lax.fori_loop(4, 4 * panels, step, 0)

    last = 2 * panels - 1
    finish(last)
    leave(last).start()

    def drain(k, carry):
        combine(k)
        return carry

    lax.fori_loop(last - LAG, last + 1, drain, 0)

    for k in (last - 1, last):
        send_partial(k).wait_send()

    remote(s_own, s_recv, xs_sem, rr_sem, peer).wait_send()
    remote(s_own, s_recv, rs_sem, rr_sem, sibling).wait()


def solution(mesh):
    def sums(a, g):
        _, n, tokens, d = a.shape
        ff = g.shape[-1]
        half, panels, strips = d // 2, n * ff // COLS, d // STRIP
        dma = pltpu.SemaphoreType.DMA
        return pl.pallas_call(
            kernel,
            out_shape=pltpu.VMEM((n, d, ff), jnp.bfloat16),
            in_specs=[pl.BlockSpec(memory_space=pl.ANY)] * 2,
            out_specs=pl.BlockSpec(memory_space=pltpu.VMEM),
            scratch_shapes=[
                pltpu.VMEM((d, tokens), jnp.bfloat16),
                pltpu.VMEM((strips, tokens, STRIP), jnp.bfloat16),
                pltpu.VMEM((G_SLOTS, tokens, COLS), jnp.bfloat16),
                pltpu.VMEM((2, half, COLS), jnp.bfloat16),
                pltpu.VMEM((half + STRIP, COLS), jnp.float32),
                pltpu.VMEM((panels, half, COLS), jnp.bfloat16),
                pltpu.VMEM((panels, half, COLS), jnp.bfloat16),
                dma((strips,)), dma((G_SLOTS,)), dma((2,)), dma((strips // 2 + 1,)), dma((2 * panels,)),
                dma, dma((2 * panels,)), dma, dma,
            ],
            compiler_params=pltpu.CompilerParams(
                collective_id=0, has_side_effects=True, vmem_limit_bytes=46 * 1024 * 1024
            ),
            name="sums",
        )(a, g)

    return jax.shard_map(
        sums, mesh=mesh, in_specs=(P(("rep", "dp")),) * 2, out_specs=P("rep"), check_vma=False
    )
```

time: 641 us -> 196 us (0.31)
  blocking collectives: 562 us -> 0 us
  Pallas kernels: 0 us -> 190 us
  matrix products: 78.6 us -> 0 us
    dot_general x1 -> x0, blocking collectives: 562 us -> none  [step(): jnp.einsum('rsntd,rsntf->rndf', a, g, preferred_element_type=jnp.float32)]
    pallas_call x0 -> x1, Pallas kernels: none -> 190 us  [sums(): pl.pallas_call(kernel, out_shape=pltpu.VMEM((n, d, ff), jnp.bfloat16), in...]
    dot_general x1 -> x0, matrix products: 78.6 us -> none  [step(): jnp.einsum('rsntd,rsntf->rndf', a, g, preferred_element_type=jnp.float32)]
where the time goes in v2:
time: 196 us
  Pallas kernels  190 us (97%)
  local copies, waits for them, and re-layouts  6.07 us (3%)
    pallas_call x1, Pallas kernels, sums(): pl.pallas_call(kernel, out_shape=pltpu.VMEM((n, d, ff), jnp.bfloat16), in...  190 us
    unnamed x1, local copies, waits for them, and re-layouts  6.07 us

profile of v2, /device:TPU:0, one launch (start us, length us, event | category | flops | bytes accessed | tf_op | source)
XLA Modules:
  0.0 195.8 jit_solution(5390718486655592088)
XLA Ops:
  0.0 189.7 %sums.1 = bf16[4,896,2304]{2,1,0:T(8,128)(2,1)S(1)} custom-call(bf16[1,4,4096,896]{3,2,1,0:T(8,128)(2,1)} %a_ref.1, bf16[1,4,4096,2304]{3,2,1,0:T(8,128)(2,1)} %g_ref.1), custom_call_target="tpu_custom_call" | custom-call | tf_op jit(solution)/shard_map/sums/pallas_call | solution.py:271
  189.7 6.1 %copy.4 = bf16[4,896,2304]{2,1,0:T(8,128)(2,1)} copy(bf16[4,896,2304]{2,1,0:T(8,128)(2,1)S(1)} %sums.1) | data formatting | bytes 33030144

commit v3 on v2

--- a/solution.py
+++ b/solution.py
@@ -10,6 +10,8 @@
 STRIP = 128
 G_SLOTS = 3
 LAG = 4
+P_RING = 4
+X_RING = 12
 
 
 def kernel(
@@ -59,7 +61,6 @@
         s_own[p, pl.ds(lo, n)] = (mine[...] + got).astype(s_own.dtype)
 
     def flip(r):
-        load_strip(0, r, r).wait()
         at[pl.ds(pl.multiple_of(r * STRIP, STRIP), STRIP)] = raw[r].T
 
     def dot(first, n, slot):
@@ -102,12 +103,13 @@
     def fill(k, carry):
         r, h = strip(k)
         i = k // 2
+
+        @pl.when(k == 0)
+        def _():
+            load_panel(0).wait()
+
+        load_strip(0, r, r).wait()
         flip(r)
-
-        @pl.when(k == 0)
-        def _():
-            load_panel(0).wait()
-
         flat[...] = dot(pl.multiple_of(r * STRIP, STRIP), STRIP, 0)
 
         @pl.when((lax.rem(k, 2) == 0) & (k < 2 * pairs))
@@ -150,16 +152,16 @@
     def send_partial(k):
         p, lo = spot(k)
         slot = lax.rem(k, 2)
-        return remote(p_send.at[slot, pl.ds(0, size)], tile(p, other + lo, size), ps_sem.at[slot], pr_sem.at[k], sibling)
+        return remote(p_send.at[slot, pl.ds(0, size)], tile(p, other + lo, size), ps_sem.at[slot], pr_sem.at[lax.rem(k, P_RING)], sibling)
 
     def finish(k):
         p, lo = spot(k)
-        remote(p_send.at[0, pl.ds(0, size)], tile(p, own + lo, size), ps_sem.at[0], pr_sem.at[k], sibling).wait_recv()
+        remote(p_send.at[0, pl.ds(0, size)], tile(p, own + lo, size), ps_sem.at[0], pr_sem.at[lax.rem(k, P_RING)], sibling).wait_recv()
         chip_sum(p, lo, size, acc.at[pl.ds(size, size)])
 
     def leave(k):
         p, lo = spot(k)
-        return exchange(p, lo, size, xr_sem.at[k])
+        return exchange(p, lo, size, xr_sem.at[lax.rem(k, X_RING)])
 
     def combine(k):
         @pl.when(k == 1)
@@ -192,6 +194,7 @@
             @pl.when(j == 0)
             def _():
                 def turn(r, c):
+                    load_strip(0, r, r).wait()
                     flip(r)
                     return c
 
@@ -281,8 +284,8 @@
                 pltpu.VMEM((half + STRIP, COLS), jnp.float32),
                 pltpu.VMEM((panels, half, COLS), jnp.bfloat16),
                 pltpu.VMEM((panels, half, COLS), jnp.bfloat16),
-                dma((strips,)), dma((G_SLOTS,)), dma((2,)), dma((strips // 2 + 1,)), dma((2 * panels,)),
-                dma, dma((2 * panels,)), dma, dma,
+                dma((strips,)), dma((G_SLOTS,)), dma((2,)), dma((strips // 2 + 1,)), dma((P_RING,)),
+                dma, dma((X_RING,)), dma, dma,
             ],
             compiler_params=pltpu.CompilerParams(
                 collective_id=0, has_side_effects=True, vmem_limit_bytes=46 * 1024 * 1024

time: 196 us -> 193 us (0.985)
  Pallas kernels: 190 us -> 187 us
    pallas_call x1, Pallas kernels: 190 us -> 187 us  [sums(): pl.pallas_call(kernel, out_shape=pltpu.VMEM((n, d, ff), jnp.bfloat16), in...]
where the time goes in v3:
time: 193 us
  Pallas kernels  187 us (97%)
  local copies, waits for them, and re-layouts  6.07 us (3%)
    pallas_call x1, Pallas kernels, sums(): pl.pallas_call(kernel, out_shape=pltpu.VMEM((n, d, ff), jnp.bfloat16), in...  187 us
    unnamed x1, local copies, waits for them, and re-layouts  6.07 us

profile of v3, /device:TPU:0, one launch (start us, length us, event | category | flops | bytes accessed | tf_op | source)
XLA Modules:
  0.0 192.6 jit_solution(4401636201401162749)
XLA Ops:
  0.0 186.5 %sums.1 = bf16[4,896,2304]{2,1,0:T(8,128)(2,1)S(1)} custom-call(bf16[1,4,4096,896]{3,2,1,0:T(8,128)(2,1)} %a_ref.1, bf16[1,4,4096,2304]{3,2,1,0:T(8,128)(2,1)} %g_ref.1), custom_call_target="tpu_custom_call" | custom-call | tf_op jit(solution)/shard_map/sums/pallas_call | solution.py:274
  186.6 6.1 %copy.4 = bf16[4,896,2304]{2,1,0:T(8,128)(2,1)} copy(bf16[4,896,2304]{2,1,0:T(8,128)(2,1)S(1)} %sums.1) | data formatting | bytes 33030144

commit v4 on v3

--- a/solution.py
+++ b/solution.py
@@ -4,6 +4,7 @@
 from jax.experimental import pallas as pl
 from jax.experimental.pallas import tpu as pltpu
 from jax.sharding import PartitionSpec as P
+
 
 MESH = pl.DeviceIdType.MESH
 COLS = 256
@@ -12,10 +13,11 @@
 LAG = 4
 P_RING = 4
 X_RING = 12
+LATE = 2
 
 
 def kernel(
-    a_ref, g_ref, out_ref,
+    a_ref, g_ref, out_ref, turn_mine, turn_other, turn_got, late_mine, late_other,
     at, raw, gs, p_send, acc, s_own, s_recv,
     a_sem, g_sem, ps_sem, p0_sem, pr_sem, xs_sem, xr_sem, rs_sem, rr_sem,
 ):
@@ -24,6 +26,7 @@
     size = half // 2
     per = cols // COLS
     panels = n_mat * per
+    early = 2 * panels - LATE - 1
     strips = rows // STRIP
     pairs = strips // 2
     rest = STRIP // 2
@@ -159,9 +162,24 @@
         remote(p_send.at[0, pl.ds(0, size)], tile(p, own + lo, size), ps_sem.at[0], pr_sem.at[lax.rem(k, P_RING)], sibling).wait_recv()
         chip_sum(p, lo, size, acc.at[pl.ds(size, size)])
 
+        @pl.when(k == early)
+        def _():
+            turn_mine[0] = s_own[p, pl.ds(lo, size)]
+            remote(turn_mine, turn_other, rs_sem, rr_sem, sibling).start()
+
+        @pl.when(k > early)
+        def _():
+            i = k - early - 1
+            late_mine[i] = s_own[p, pl.ds(lo, size)]
+            remote(late_mine.at[i], late_other.at[i], rs_sem, rr_sem, sibling).start()
+
     def leave(k):
         p, lo = spot(k)
         return exchange(p, lo, size, xr_sem.at[lax.rem(k, X_RING)])
+
+    def leave_unfinished():
+        p, lo = early // 2, early % 2 * size
+        return remote(s_own.at[p, pl.ds(lo, size)], turn_got.at[0], xs_sem, xr_sem.at[early % X_RING], peer)
 
     def combine(k):
         @pl.when(k == 1)
@@ -232,9 +250,13 @@
         def _():
             send_partial(k).start()
 
-        @pl.when((t == 0) & (k >= 3))
+        @pl.when((t == 0) & (k >= 3) & (k <= early))
         def _():
             leave(k - 1).start()
+
+        @pl.when((t == 0) & (k == early + 1))
+        def _():
+            leave_unfinished().start()
 
         @pl.when((t == 1) & (b == 1) & (p + G_SLOTS < panels))
         def _():
@@ -250,19 +272,59 @@
 
     last = 2 * panels - 1
     finish(last)
-    leave(last).start()
 
     def drain(k, carry):
         combine(k)
         return carry
 
-    lax.fori_loop(last - LAG, last + 1, drain, 0)
+    lax.fori_loop(last - LAG, early, drain, 0)
 
     for k in (last - 1, last):
         send_partial(k).wait_send()
 
-    remote(s_own, s_recv, xs_sem, rr_sem, peer).wait_send()
+    full = (early + 1) // 2
+    remote(s_own.at[pl.ds(0, full)], s_recv.at[pl.ds(0, full)], xs_sem, rr_sem, peer).wait_send()
+    if early % 2 == 0:
+        exchange(full, 0, size, rr_sem).wait_send()
     remote(s_own, s_recv, rs_sem, rr_sem, sibling).wait()
+    leave_unfinished().wait_recv()
+
+
+def copy_out(x_ref, o_ref, sem):
+    n, rows, _ = x_ref.shape
+    size = rows // 4
+    copies = []
+    for i in range(n):
+        for j in range(4):
+            part = (i, pl.ds(j * size, size))
+            copies.append(pltpu.make_async_copy(x_ref.at[part], o_ref.at[part], sem.at[i, j]))
+    for c in copies:
+        c.start()
+    for c in copies:
+        c.wait()
+
+
+def add_late(so_far, *refs):
+    *terms, o_ref, buf, sem = refs
+    n_mat, rows, cols = o_ref.shape
+    size = rows // 4
+    per = cols // COLS
+    core = lax.rem(lax.axis_index("dp"), 2)
+    copies = []
+    for i in range(LATE + 1):
+        k = 2 * n_mat * per - LATE - 1 + i
+        p, b = divmod(k, 2)
+        n, j = divmod(p, per)
+        group, at = terms[4 * min(i, 1) :][:4], max(i - 1, 0)
+        for h in range(2):
+            ours, theirs = group[h][at].astype(jnp.float32), group[2 + h][at].astype(jnp.float32)
+            buf[h, i] = (ours + theirs).astype(buf.dtype)
+            first = pl.multiple_of((core + (1 - 2 * core) * h) * 2 * size + b * size, size)
+            there = o_ref.at[n, pl.ds(first, size), pl.ds(j * COLS, COLS)]
+            copies.append(pltpu.make_async_copy(buf.at[h, i], there, sem.at[h, i]))
+            copies[-1].start()
+    for c in copies:
+        c.wait()
 
 
 def solution(mesh):
@@ -271,11 +333,16 @@
         ff = g.shape[-1]
         half, panels, strips = d // 2, n * ff // COLS, d // STRIP
         dma = pltpu.SemaphoreType.DMA
-        return pl.pallas_call(
+        block = (half // 2, COLS)
+        turn, late = (pltpu.VMEM((i, *block), jnp.bfloat16) for i in (1, LATE))
+        cross, across = [(0, 2), (2, 0), (1, 3), (3, 1)], [(0, 1), (1, 0), (2, 3), (3, 2)]
+        vmem, hbm = pl.BlockSpec(memory_space=pltpu.VMEM), pl.BlockSpec(memory_space=pltpu.HBM)
+        result = jax.ShapeDtypeStruct((n, d, ff), jnp.bfloat16)
+        most, turn_mine, turn_other, turn_got, late_mine, late_other = pl.pallas_call(
             kernel,
-            out_shape=pltpu.VMEM((n, d, ff), jnp.bfloat16),
+            out_shape=(pltpu.VMEM((n, d, ff), jnp.bfloat16), turn, turn, turn, late, late),
             in_specs=[pl.BlockSpec(memory_space=pl.ANY)] * 2,
-            out_specs=pl.BlockSpec(memory_space=pltpu.VMEM),
+            out_specs=(vmem,) * 6,
             scratch_shapes=[
                 pltpu.VMEM((d, tokens), jnp.bfloat16),
                 pltpu.VMEM((strips, tokens, STRIP), jnp.bfloat16),
@@ -292,6 +359,33 @@
             ),
             name="sums",
         )(a, g)
+        late_got = lax.ppermute(late_mine, "dp", cross)
+        turn_got_other = lax.ppermute(turn_got, "dp", across)
+        out = pl.pallas_call(
+            copy_out,
+            out_shape=result,
+            in_specs=[vmem],
+            out_specs=hbm,
+            scratch_shapes=[dma((n, 4))],
+            compiler_params=pltpu.CompilerParams(vmem_limit_bytes=1024 * 1024),
+            cost_estimate=pl.CostEstimate(flops=10**10, bytes_accessed=2 * n * d * ff, transcendentals=0),
+            name="copy_out",
+        )(most)
+        late_got_other = lax.ppermute(late_got, "dp", across)
+        return pl.pallas_call(
+            add_late,
+            out_shape=result,
+            in_specs=[hbm] + [vmem] * 8,
+            out_specs=hbm,
+            scratch_shapes=[pltpu.VMEM((2, LATE + 1, *block), jnp.bfloat16), dma((2, LATE + 1))],
+            input_output_aliases={0: 0},
+            compiler_params=pltpu.CompilerParams(vmem_limit_bytes=4 * 1024 * 1024),
+            name="add_late",
+        )(
+            out,
+            *(turn_mine, turn_other, turn_got, turn_got_other),
+            *(late_mine, late_other, late_got, late_got_other),
+        )
 
     return jax.shard_map(
         sums, mesh=mesh, in_specs=(P(("rep", "dp")),) * 2, out_specs=P("rep"), check_vma=False

time: 193 us -> 195 us (1.010)
  waiting for transfers between devices: 0 us -> 7.22 us
  local copies, waits for them, and re-layouts: 6.07 us -> 0 us
    ppermute x0 -> x3, waiting for transfers between devices: none -> 7.22 us  [the longest x1 7.21 us: sums(): late_got = lax.ppermute(late_mine, 'dp', cross)]
    unnamed x1 -> x0, local copies, waits for them, and re-layouts: 6.07 us -> none
    pallas_call x1 -> x3, Pallas kernels: 187 us -> 187 us  [the longest x1 181 us: sums(): pl.pallas_call(kernel, out_shape=(pltpu.VMEM((n, d, ff), jnp.bfloat16), t...]
  transfers between devices with their start and end apart: 0 -> 3, of which waited for: 0 -> 1; matrix products, arithmetic and copies ran while one was open for 0% -> 0% of each run, Pallas kernels for 0% -> 3%
where the time goes in v4:
time: 195 us
  Pallas kernels  187 us (96%)
  waiting for transfers between devices  7.22 us (4%)
    pallas_call x1, Pallas kernels, sums(): pl.pallas_call(kernel, out_shape=(pltpu.VMEM((n, d, ff), jnp.bfloat16), t...  181 us
    ppermute x1, waiting for transfers between devices, sums(): late_got = lax.ppermute(late_mine, 'dp', cross)  7.21 us
    pallas_call x1, Pallas kernels, sums(): pl.pallas_call(copy_out, out_shape=result, in_specs=[vmem], out_specs=hbm...  5.9 us
  transfers between devices with their start and end apart: 3, of which 1 were waited for; matrix products, arithmetic and copies ran while one was open for 0% of the time, Pallas kernels for 3%

profile of v4, /device:TPU:0, one launch (start us, length us, event | category | flops | bytes accessed | tf_op | source)
XLA Modules:
  0.0 194.8 jit_solution(17285161020340191512)
XLA Ops:
  0.0 180.6 %sums.1 = (bf16[4,896,2304]{2,1,0:T(8,128)(2,1)S(1)}, bf16[1,224,256]{2,1,0:T(8,128)(2,1)S(1)}, bf16[1,224,256]{2,1,0:T(8,128)(2,1)S(1)}, bf16[1,224,256]{2,1,0:...) custom-call(bf16[1,4,4096,896]{3,2,1,0:T(8,128)(2,1)} %a_ref.1, ...), custom_call_target="tpu_custom_call" | custom-call | tf_op jit(solution)/shard_map/sums/pallas_call | solution.py:341
  180.6 0.0 collective-permute-start.1
  180.7 0.0 collective-permute-start
  180.7 7.2 %collective-permute-done.1.refs_6_ = bf16[2,224,256]{2,1,0:T(8,128)(2,1)S(1)} collective-permute-done((bf16[2,224,256]{2,1,0:T(8,128)(2,1)S(1)}, bf16[2,224,256]{2,1,0:T(8,128)(2,1)S(1)}, u32[]{:S(2)}, u32[]{:S(2)}) %collective-permute-start.1) | collective-permute-done | bytes 229408 | tf_op jit(solution)/shard_map/ppermute | solution.py:362
  187.9 0.0 collective-permute-start.2
  187.9 5.9 %copy_out.1.so_far = bf16[4,896,2304]{2,1,0:T(8,128)(2,1)} custom-call(bf16[4,896,2304]{2,1,0:T(8,128)(2,1)S(1)} %get-tuple-element.11.x_ref), custom_call_target="tpu_custom_call" | custom-call | flops 10000000000 | bytes 16515072 | tf_op jit(solution)/shard_map/copy_out/pallas_call | solution.py:364
  193.8 0.0 collective-permute-done.refs_3_
  193.8 0.0 collective-permute-done.2.refs_7_
  193.8 0.9 add_late.1
Async XLA Ops:
  180.6 7.3 %collective-permute-start.1 = (bf16[2,224,256]{2,1,0:T(8,128)(2,1)S(1)}, bf16[2,224,256]{2,1,0:T(8,128)(2,1)S(1)}, u32[]{:S(2)}, u32[]{:S(2)}) collective-permute-start(bf16[2,224,256]{2,1,0:T(8,128)(2,1)S(1)} %get-tuple-element.15.refs_4_), channel_id=1, source_target_pairs={{0,2},{2,0},{1,3},{3,1},{4,6},{6,4},{5,7},{7,5}} | collective-permute-start | bytes 688136 | tf_op jit(solution)/shard_map/ppermute | solution.py:362
  180.7 13.2 %collective-permute-start = (bf16[1,224,256]{2,1,0:T(8,128)(2,1)S(1)}, bf16[1,224,256]{2,1,0:T(8,128)(2,1)S(1)}, u32[]{:S(2)}, u32[]{:S(2)}) collective-permute-start(bf16[1,224,256]{2,1,0:T(8,128)(2,1)S(1)} %get-tuple-element.14.refs_2_), channel_id=1, source_target_pairs={{0,1},{1,0},{2,3},{3,2},{4,5},{5,4},{6,7},{7,6}} | collective-permute-start | bytes 344072 | tf_op jit(solution)/shard_map/ppermute | solution.py:363
  187.9 5.9 %collective-permute-start.2 = (bf16[2,224,256]{2,1,0:T(8,128)(2,1)S(1)}, bf16[2,224,256]{2,1,0:T(8,128)(2,1)S(1)}, u32[]{:S(2)}, u32[]{:S(2)}) collective-permute-start(bf16[2,224,256]{2,1,0:T(8,128)(2,1)S(1)} %collective-permute-done.1.refs_6_), channel_id=1, source_target_pairs={{0,1},{1,0},{2,3},{3,2},{4,5},{5,4},{6,7},{7,6}} | collective-permute-start | bytes 688136 | tf_op jit(solution)/shard_map/ppermute | solution.py:374

commit v5 on v3

--- a/solution.py
+++ b/solution.py
@@ -1,3 +1,5 @@
+import functools
+
 import jax
 import jax.numpy as jnp
 from jax import lax
@@ -5,17 +7,19 @@
 from jax.experimental.pallas import tpu as pltpu
 from jax.sharding import PartitionSpec as P
 
+
 MESH = pl.DeviceIdType.MESH
 COLS = 256
 STRIP = 128
 G_SLOTS = 3
-LAG = 4
+LAG = 2
 P_RING = 4
-X_RING = 12
+X_RING = 8
+SPLIT = 4
 
 
 def kernel(
-    a_ref, g_ref, out_ref,
+    a_ref, g_ref, out_ref, turn_got, turn_mine, turn_other, late_mine, late_other,
     at, raw, gs, p_send, acc, s_own, s_recv,
     a_sem, g_sem, ps_sem, p0_sem, pr_sem, xs_sem, xr_sem, rs_sem, rr_sem,
 ):
@@ -24,6 +28,7 @@
     size = half // 2
     per = cols // COLS
     panels = n_mat * per
+    turn = panels - 2
     strips = rows // STRIP
     pairs = strips // 2
     rest = STRIP // 2
@@ -158,29 +163,47 @@
         p, lo = spot(k)
         remote(p_send.at[0, pl.ds(0, size)], tile(p, own + lo, size), ps_sem.at[0], pr_sem.at[lax.rem(k, P_RING)], sibling).wait_recv()
         chip_sum(p, lo, size, acc.at[pl.ds(size, size)])
+        here = pl.ds(lo, size)
+        for i, (mine, other) in enumerate(((turn_mine, turn_other), (late_mine, late_other))):
+
+            @pl.when(p == turn + i)
+            def _(mine=mine, other=other):
+                mine[here] = s_own[p, here]
+                remote(mine.at[here], other.at[here], rs_sem, rr_sem, sibling).start()
+
+    def arrival(p):
+        return xr_sem.at[lax.rem(p, X_RING)]
 
     def leave(k):
         p, lo = spot(k)
-        return exchange(p, lo, size, xr_sem.at[lax.rem(k, X_RING)])
-
-    def combine(k):
-        @pl.when(k == 1)
-        def _():
-            exchange(0, 0, half, xr_sem.at[0]).wait_recv()
-
-        @pl.when(k > 1)
-        def _():
-            leave(k).wait_recv()
-
-        def one(k, c):
-            p, lo = spot(k)
+
+        @pl.when(p < SPLIT)
+        def _():
+            exchange(p, lo, size, arrival(p)).start()
+
+        @pl.when((lo > 0) & (p >= SPLIT) & (p < turn))
+        def _():
+            exchange(p, 0, half, arrival(p)).start()
+
+        @pl.when((lo > 0) & (p == turn))
+        def _():
+            leave_unfinished().start()
+
+    def leave_unfinished():
+        return remote(s_own.at[turn], turn_got, xs_sem, xr_sem.at[turn % X_RING], peer)
+
+    def combine(p):
+        exchange(p, 0, half, arrival(p)).wait_recv()
+
+        def one(b, c):
+            lo = pl.multiple_of(b * size, size)
             both = s_own[p, pl.ds(lo, size)].astype(jnp.float32) + s_recv[p, pl.ds(lo, size)].astype(jnp.float32)
             here = tile(p, own + lo, size)
             here[...] = both.astype(out_ref.dtype)
             remote(here, here, rs_sem, rr_sem, sibling).start()
             return c
 
-        lax.fori_loop(k - 1 // k, k + 1, one, 0)
+        lax.fori_loop(0, 2, one, 0)
 
     def step(q, carry):
         k, t = q // 2, lax.rem(q, 2)
@@ -224,45 +247,71 @@
 
             p_send[lax.rem(k, 2), pl.ds(0, size)] = acc[pl.ds(0, size)].astype(p_send.dtype)
 
-        @pl.when((t == 0) & (k >= 3))
-        def _():
-            finish(k - 1)
-
         @pl.when(t == 0)
         def _():
             send_partial(k).start()
 
-        @pl.when((t == 0) & (k >= 3))
-        def _():
-            leave(k - 1).start()
-
         @pl.when((t == 1) & (b == 1) & (p + G_SLOTS < panels))
         def _():
             load_panel(p + G_SLOTS).start()
 
-        @pl.when((t == 1) & (k - 1 - LAG >= 1))
-        def _():
-            combine(k - 1 - LAG)
+        @pl.when(t == 1)
+        def _():
+            finish(k)
+            leave(k)
+
+        @pl.when((t == 1) & (b == 1) & (p >= LAG))
+        def _():
+            combine(p - LAG)
 
         return carry
 
     lax.fori_loop(4, 4 * panels, step, 0)
 
-    last = 2 * panels - 1
-    finish(last)
-    leave(last).start()
-
-    def drain(k, carry):
-        combine(k)
+    def drain(p, carry):
+        combine(p)
         return carry
 
-    lax.fori_loop(last - LAG, last + 1, drain, 0)
-
-    for k in (last - 1, last):
+    lax.fori_loop(panels - LAG, turn, drain, 0)
+
+    for k in (2 * panels - 2, 2 * panels - 1):
         send_partial(k).wait_send()
 
-    remote(s_own, s_recv, xs_sem, rr_sem, peer).wait_send()
+    sent = pl.ds(0, turn + 1)
+    remote(s_own.at[sent], s_recv.at[sent], xs_sem, rr_sem, peer).wait_send()
     remote(s_own, s_recv, rs_sem, rr_sem, sibling).wait()
+    leave_unfinished().wait_recv()
+
+
+def copy_out(x_ref, o_ref, sem):
+    n, rows, _ = x_ref.shape
+    size = rows // 4
+    copies = []
+    for i in range(n):
+        for j in range(4):
+            part = (i, pl.ds(j * size, size))
+            copies.append(pltpu.make_async_copy(x_ref.at[part], o_ref.at[part], sem.at[i, j]))
+    for c in copies:
+        c.start()
+    for c in copies:
+        c.wait()
+
+
+def add_panel(back, so_far, mine, got, other, got_other, o_ref, buf, sem):
+    n_mat, rows, cols = o_ref.shape
+    half = rows // 2
+    per = cols // COLS
+    n, j = divmod(n_mat * per - back, per)
+    core = lax.rem(lax.axis_index("dp"), 2)
+    copies = []
+    for h, (ours, theirs) in enumerate(((mine, got), (other, got_other))):
+        buf[h] = (ours[...].astype(jnp.float32) + theirs[...].astype(jnp.float32)).astype(buf.dtype)
+        first = pl.multiple_of((core + (1 - 2 * core) * h) * half, half)
+        there = o_ref.at[n, pl.ds(first, half), pl.ds(j * COLS, COLS)]
+        copies.append(pltpu.make_async_copy(buf.at[h], there, sem.at[h]))
+        copies[-1].start()
+    for c in copies:
+        c.wait()
 
 
 def solution(mesh):
@@ -271,11 +320,15 @@
         ff = g.shape[-1]
         half, panels, strips = d // 2, n * ff // COLS, d // STRIP
         dma = pltpu.SemaphoreType.DMA
-        return pl.pallas_call(
+        block = (half, COLS)
+        cross, across = [(0, 2), (2, 0), (1, 3), (3, 1)], [(0, 1), (1, 0), (2, 3), (3, 2)]
+        vmem, hbm = pl.BlockSpec(memory_space=pltpu.VMEM), pl.BlockSpec(memory_space=pltpu.HBM)
+        result = jax.ShapeDtypeStruct((n, d, ff), jnp.bfloat16)
+        most, turn_got, turn_mine, turn_other, late_mine, late_other = pl.pallas_call(
             kernel,
-            out_shape=pltpu.VMEM((n, d, ff), jnp.bfloat16),
+            out_shape=(pltpu.VMEM((n, d, ff), jnp.bfloat16), *[pltpu.VMEM(block, jnp.bfloat16)] * 5),
             in_specs=[pl.BlockSpec(memory_space=pl.ANY)] * 2,
-            out_specs=pl.BlockSpec(memory_space=pltpu.VMEM),
+            out_specs=(vmem,) * 6,
             scratch_shapes=[
                 pltpu.VMEM((d, tokens), jnp.bfloat16),
                 pltpu.VMEM((strips, tokens, STRIP), jnp.bfloat16),
@@ -293,6 +346,34 @@
             name="sums",
         )(a, g)
 
+        def add(back, out, *terms):
+            return pl.pallas_call(
+                functools.partial(add_panel, back),
+                out_shape=result,
+                in_specs=[hbm] + [vmem] * 4,
+                out_specs=hbm,
+                scratch_shapes=[pltpu.VMEM((2, *block), jnp.bfloat16), dma((2,))],
+                input_output_aliases={0: 0},
+                compiler_params=pltpu.CompilerParams(vmem_limit_bytes=4 * 1024 * 1024),
+                name="add_panel",
+            )(out, *terms)
+
+        late_got = lax.ppermute(late_mine, "dp", cross)
+        turn_got_other = lax.ppermute(turn_got, "dp", across)
+        out = pl.pallas_call(
+            copy_out,
+            out_shape=result,
+            in_specs=[vmem],
+            out_specs=hbm,
+            scratch_shapes=[dma((n, 4))],
+            compiler_params=pltpu.CompilerParams(vmem_limit_bytes=1024 * 1024),
+            cost_estimate=pl.CostEstimate(flops=10**10, bytes_accessed=2 * n * d * ff, transcendentals=0),
+            name="copy_out",
+        )(most)
+        out = add(2, out, turn_mine, turn_got, turn_other, turn_got_other)
+        late_got_other = lax.ppermute(late_got, "dp", across)
+        return add(1, out, late_mine, late_got, late_other, late_got_other)
+
     return jax.shard_map(
         sums, mesh=mesh, in_specs=(P(("rep", "dp")),) * 2, out_specs=P("rep"), check_vma=False
     )

time: 193 us -> 195 us (1.010)
  waiting for transfers between devices: 0 us -> 7.1 us
  local copies, waits for them, and re-layouts: 6.07 us -> 0 us
    ppermute x0 -> x3, waiting for transfers between devices: none -> 7.1 us  [the longest x1 7.1 us: sums(): late_got = lax.ppermute(late_mine, 'dp', cross)]
    unnamed x1 -> x0, local copies, waits for them, and re-layouts: 6.07 us -> none
    pallas_call x1 -> x4, Pallas kernels: 187 us -> 188 us  [the longest x1 180 us: sums(): pl.pallas_call(kernel, out_shape=(pltpu.VMEM((n, d, ff), jnp.bfloat16), *...]
  transfers between devices with their start and end apart: 0 -> 3, of which waited for: 0 -> 1; matrix products, arithmetic and copies ran while one was open for 0% -> 0% of each run, Pallas kernels for 0% -> 3%
where the time goes in v5:
time: 195 us
  Pallas kernels  188 us (96%)
  waiting for transfers between devices  7.1 us (4%)
    pallas_call x1, Pallas kernels, sums(): pl.pallas_call(kernel, out_shape=(pltpu.VMEM((n, d, ff), jnp.bfloat16), *...  180 us
    ppermute x1, waiting for transfers between devices, sums(): late_got = lax.ppermute(late_mine, 'dp', cross)  7.1 us
    pallas_call x1, Pallas kernels, sums(): pl.pallas_call(copy_out, out_shape=result, in_specs=[vmem], out_specs=hbm...  5.9 us
  transfers between devices with their start and end apart: 3, of which 1 were waited for; matrix products, arithmetic and copies ran while one was open for 0% of the time, Pallas kernels for 3%

profile of v5, /device:TPU:0, one launch (start us, length us, event | category | flops | bytes accessed | tf_op | source)
XLA Modules:
  0.0 194.9 jit_solution(9775024612696010664)
XLA Ops:
  0.0 180.1 %sums.1 = (bf16[4,896,2304]{2,1,0:T(8,128)(2,1)S(1)}, bf16[448,256]{1,0:T(8,128)(2,1)S(1)}, bf16[448,256]{1,0:T(8,128)(2,1)S(1)}, bf16[448,256]{1,0:T(8,128)(2,1...) custom-call(bf16[1,4,4096,896]{3,2,1,0:T(8,128)(2,1)} %a_ref.1, bf16[1,4,4096,2304]{3,2,1,0:T(8,128)(2,1)} %g_ref.1), custom_call_target="tpu_custom_call" | custom-call | tf_op jit(solution)/shard_map/sums/pallas_call | solution.py:327
  180.1 0.0 collective-permute-start.1
  180.1 0.0 collective-permute-start
  180.2 7.1 %collective-permute-done.1.got = bf16[448,256]{1,0:T(8,128)(2,1)S(1)} collective-permute-done((bf16[448,256]{1,0:T(8,128)(2,1)S(1)}, bf16[448,256]{1,0:T(8,128)(2,1)S(1)}, u32[]{:S(2)}, u32[]{:S(2)}) %collective-permute-start.1) | collective-permute-done | bytes 229408 | tf_op jit(solution)/shard_map/ppermute | solution.py:361
  187.3 0.0 collective-permute-start.2
  187.3 5.9 %copy_out.1.so_far = bf16[4,896,2304]{2,1,0:T(8,128)(2,1)} custom-call(bf16[4,896,2304]{2,1,0:T(8,128)(2,1)S(1)} %get-tuple-element.11.x_ref), custom_call_target="tpu_custom_call" | custom-call | flops 10000000000 | bytes 16515072 | tf_op jit(solution)/shard_map/copy_out/pallas_call | solution.py:363
  193.2 0.0 collective-permute-done.got_other
  193.2 0.8 add_panel.2.so_far
  194.0 0.0 collective-permute-done.2.got_other
  194.1 0.8 add_panel.3
Async XLA Ops:
  180.1 7.2 %collective-permute-start.1 = (bf16[448,256]{1,0:T(8,128)(2,1)S(1)}, bf16[448,256]{1,0:T(8,128)(2,1)S(1)}, u32[]{:S(2)}, u32[]{:S(2)}) collective-permute-start(bf16[448,256]{1,0:T(8,128)(2,1)S(1)} %get-tuple-element.15.mine), channel_id=1, source_target_pairs={{0,2},{2,0},{1,3},{3,1},{4,6},{6,4},{5,7},{7,5}} | collective-permute-start | bytes 688136 | tf_op jit(solution)/shard_map/ppermute | solution.py:361
  180.1 13.0 %collective-permute-start = (bf16[448,256]{1,0:T(8,128)(2,1)S(1)}, bf16[448,256]{1,0:T(8,128)(2,1)S(1)}, u32[]{:S(2)}, u32[]{:S(2)}) collective-permute-start(bf16[448,256]{1,0:T(8,128)(2,1)S(1)} %get-tuple-element.13.got), channel_id=1, source_target_pairs={{0,1},{1,0},{2,3},{3,2},{4,5},{5,4},{6,7},{7,6}} | collective-permute-start | bytes 688136 | tf_op jit(solution)/shard_map/ppermute | solution.py:362
  187.3 6.8 %collective-permute-start.2 = (bf16[448,256]{1,0:T(8,128)(2,1)S(1)}, bf16[448,256]{1,0:T(8,128)(2,1)S(1)}, u32[]{:S(2)}, u32[]{:S(2)}) collective-permute-start(bf16[448,256]{1,0:T(8,128)(2,1)S(1)} %collective-permute-done.1.got), channel_id=1, source_target_pairs={{0,1},{1,0},{2,3},{3,2},{4,5},{5,4},{6,7},{7,6}} | collective-permute-start | bytes 688136 | tf_op jit(solution)/shard_map/ppermute | solution.py:374

commit v6 on v5

--- a/solution.py
+++ b/solution.py
@@ -12,23 +12,23 @@
 COLS = 256
 STRIP = 128
 G_SLOTS = 3
-LAG = 2
+LAG = 4
 P_RING = 4
-X_RING = 8
+X_RING = 12
 SPLIT = 4
 
 
 def kernel(
-    a_ref, g_ref, out_ref, turn_got, turn_mine, turn_other, late_mine, late_other,
+    a_ref, g_ref, out_ref, got, mine0, other0, mine1, other1, mine2, other2,
     at, raw, gs, p_send, acc, s_own, s_recv,
-    a_sem, g_sem, ps_sem, p0_sem, pr_sem, xs_sem, xr_sem, rs_sem, rr_sem,
+    a_sem, g_sem, ps_sem, p0_sem, pr_sem, xs_sem, xr_sem, rs_sem, rr_sem, o_sem,
 ):
     n_mat, rows, cols = out_ref.shape
     half = rows // 2
     size = half // 2
     per = cols // COLS
     panels = n_mat * per
-    turn = panels - 2
+    turn = panels - 3
     strips = rows // STRIP
     pairs = strips // 2
     rest = STRIP // 2
@@ -164,12 +164,12 @@
         remote(p_send.at[0, pl.ds(0, size)], tile(p, own + lo, size), ps_sem.at[0], pr_sem.at[lax.rem(k, P_RING)], sibling).wait_recv()
         chip_sum(p, lo, size, acc.at[pl.ds(size, size)])
         here = pl.ds(lo, size)
-        for i, (mine, other) in enumerate(((turn_mine, turn_other), (late_mine, late_other))):
+        for i, (mine, other) in enumerate(((mine0, other0), (mine1, other1), (mine2, other2))):
 
             @pl.when(p == turn + i)
             def _(mine=mine, other=other):
                 mine[here] = s_own[p, here]
-                remote(mine.at[here], other.at[here], rs_sem, rr_sem, sibling).start()
+                remote(mine.at[here], other.at[here], rs_sem, rr_sem if i else o_sem, sibling).start()
 
     def arrival(p):
         return xr_sem.at[lax.rem(p, X_RING)]
@@ -185,12 +185,20 @@
         def _():
             exchange(p, 0, half, arrival(p)).start()
 
+        @pl.when((lo > 0) & (p == turn) & (core == 1))
+        def _():
+            alone(s_own.at[turn], 0).start()
+
         @pl.when((lo > 0) & (p == turn))
         def _():
-            leave_unfinished().start()
-
-    def leave_unfinished():
-        return remote(s_own.at[turn], turn_got, xs_sem, xr_sem.at[turn % X_RING], peer)
+            remote(mine0, other0, rs_sem, o_sem, sibling).wait_recv()
+
+        @pl.when((lo > 0) & (p == turn) & (core == 1))
+        def _():
+            alone(other0, 1).start()
+
+    def alone(src, i):
+        return remote(src, got.at[i], xs_sem, xr_sem.at[turn % X_RING], peer)
 
     def combine(p):
         exchange(p, 0, half, arrival(p)).wait_recv()
@@ -260,7 +268,7 @@
             finish(k)
             leave(k)
 
-        @pl.when((t == 1) & (b == 1) & (p >= LAG))
+        @pl.when((t == 1) & (b == 1) & (p >= LAG) & (p < turn + LAG))
         def _():
             combine(p - LAG)
 
@@ -272,15 +280,19 @@
         combine(p)
         return carry
 
-    lax.fori_loop(panels - LAG, turn, drain, 0)
+    lax.fori_loop(min(panels - LAG, turn), turn, drain, 0)
 
     for k in (2 * panels - 2, 2 * panels - 1):
         send_partial(k).wait_send()
 
-    sent = pl.ds(0, turn + 1)
-    remote(s_own.at[sent], s_recv.at[sent], xs_sem, rr_sem, peer).wait_send()
-    remote(s_own, s_recv, rs_sem, rr_sem, sibling).wait()
-    leave_unfinished().wait_recv()
+    remote(s_own.at[pl.ds(0, turn)], s_recv.at[pl.ds(0, turn)], xs_sem, rr_sem, peer).wait_send()
+    remote(s_own, s_recv, rs_sem, rr_sem, sibling).wait_send()
+    rest_of = pl.ds(0, panels - 1)
+    remote(s_own.at[rest_of], s_recv.at[rest_of], rs_sem, rr_sem, sibling).wait_recv()
+
+    @pl.when(core == 1)
+    def _():
+        remote(got, got, xs_sem, xr_sem.at[turn % X_RING], peer).wait()
 
 
 def copy_out(x_ref, o_ref, sem):
@@ -314,6 +326,42 @@
         c.wait()
 
 
+def add_two(so_far, mine0, other0, mine1, other1, got, got_other, late, late_other, o_ref, buf, sem):
+    n_mat, rows, cols = o_ref.shape
+    half = rows // 2
+    per = cols // COLS
+    core = lax.rem(lax.axis_index("dp"), 2)
+
+    def put(to, ours, theirs):
+        to[...] = (ours[...].astype(jnp.float32) + theirs[...].astype(jnp.float32)).astype(buf.dtype)
+
+    def copy(i, h):
+        n, j = divmod(n_mat * per - 3 + i, per)
+        row = pl.multiple_of((core + (1 - 2 * core) * h) * half, half)
+        there = o_ref.at[n, pl.ds(row, half), pl.ds(j * COLS, COLS)]
+        return pltpu.make_async_copy(buf.at[i, h], there, sem.at[i, h])
+
+    put(buf.at[1, 0], mine1, late)
+    put(buf.at[1, 1], other1, late_other)
+
+    @pl.when(core == 0)
+    def _():
+        put(buf.at[0, 0], mine0, got_other.at[1])
+        put(buf.at[0, 1], other0, got_other.at[0])
+
+    @pl.when(core == 1)
+    def _():
+        put(buf.at[0, 0], mine0, got.at[0])
+        put(buf.at[0, 1], other0, got.at[1])
+
+    for i in range(2):
+        for h in range(2):
+            copy(i, h).start()
+    for i in range(2):
+        for h in range(2):
+            copy(i, h).wait()
+
+
 def solution(mesh):
     def sums(a, g):
         _, n, tokens, d = a.shape
@@ -324,11 +372,11 @@
         cross, across = [(0, 2), (2, 0), (1, 3), (3, 1)], [(0, 1), (1, 0), (2, 3), (3, 2)]
         vmem, hbm = pl.BlockSpec(memory_space=pltpu.VMEM), pl.BlockSpec(memory_space=pltpu.HBM)
         result = jax.ShapeDtypeStruct((n, d, ff), jnp.bfloat16)
-        most, turn_got, turn_mine, turn_other, late_mine, late_other = pl.pallas_call(
+        most, got, *late = pl.pallas_call(
             kernel,
-            out_shape=(pltpu.VMEM((n, d, ff), jnp.bfloat16), *[pltpu.VMEM(block, jnp.bfloat16)] * 5),
+            out_shape=(pltpu.VMEM((n, d, ff), jnp.bfloat16), pltpu.VMEM((2, *block), jnp.bfloat16), *[pltpu.VMEM(block, jnp.bfloat16)] * 6),
             in_specs=[pl.BlockSpec(memory_space=pl.ANY)] * 2,
-            out_specs=(vmem,) * 6,
+            out_specs=(vmem,) * 8,
             scratch_shapes=[
                 pltpu.VMEM((d, tokens), jnp.bfloat16),
                 pltpu.VMEM((strips, tokens, STRIP), jnp.bfloat16),
@@ -338,28 +386,29 @@
                 pltpu.VMEM((panels, half, COLS), jnp.bfloat16),
                 pltpu.VMEM((panels, half, COLS), jnp.bfloat16),
                 dma((strips,)), dma((G_SLOTS,)), dma((2,)), dma((strips // 2 + 1,)), dma((P_RING,)),
-                dma, dma((X_RING,)), dma, dma,
+                dma, dma((X_RING,)), dma, dma, dma,
             ],
             compiler_params=pltpu.CompilerParams(
                 collective_id=0, has_side_effects=True, vmem_limit_bytes=46 * 1024 * 1024
             ),
             name="sums",
         )(a, g)
-
-        def add(back, out, *terms):
+        mine, other = late[::2], late[1::2]
+
+        def local(body, n_terms, bufs, sems):
             return pl.pallas_call(
-                functools.partial(add_panel, back),
+                body,
                 out_shape=result,
-                in_specs=[hbm] + [vmem] * 4,
+                in_specs=[hbm] + [vmem] * n_terms,
                 out_specs=hbm,
-                scratch_shapes=[pltpu.VMEM((2, *block), jnp.bfloat16), dma((2,))],
+                scratch_shapes=[pltpu.VMEM((*bufs, *block), jnp.bfloat16), dma(sems)],
                 input_output_aliases={0: 0},
                 compiler_params=pltpu.CompilerParams(vmem_limit_bytes=4 * 1024 * 1024),
-                name="add_panel",
-            )(out, *terms)
-
-        late_got = lax.ppermute(late_mine, "dp", cross)
-        turn_got_other = lax.ppermute(turn_got, "dp", across)
+                name="add",
+            )
+
+        late0 = lax.ppermute(mine[1], "dp", cross)
+        late1 = lax.ppermute(mine[2], "dp", cross)
         out = pl.pallas_call(
             copy_out,
             out_shape=result,
@@ -370,9 +419,13 @@
             cost_estimate=pl.CostEstimate(flops=10**10, bytes_accessed=2 * n * d * ff, transcendentals=0),
             name="copy_out",
         )(most)
-        out = add(2, out, turn_mine, turn_got, turn_other, turn_got_other)
-        late_got_other = lax.ppermute(late_got, "dp", across)
-        return add(1, out, late_mine, late_got, late_other, late_got_other)
+        got_other = lax.ppermute(got, "dp", across)
+        late0_other = lax.ppermute(late0, "dp", across)
+        late1_other = lax.ppermute(late1, "dp", across)
+        out = local(add_two, 8, (2, 2), (2, 2))(
+            out, mine[0], other[0], mine[1], other[1], got, got_other, late0, late0_other
+        )
+        return local(functools.partial(add_panel, 1), 4, (2,), (2,))(out, mine[2], late1, other[2], late1_other)
 
     return jax.shard_map(
         sums, mesh=mesh, in_specs=(P(("rep", "dp")),) * 2, out_specs=P("rep"), check_vma=False

time: 195 us -> 193 us (0.990)
  starting transfers between devices: 0.06 us -> 10.9 us
  Pallas kernels: 188 us -> 180 us
  waiting for transfers between devices: 7.1 us -> 2.3 us
    ppermute x3 -> x5, starting transfers between devices: 0.06 us -> 10.9 us  [the longest x1 4.39 us: sums(): late0_other = lax.ppermute(late0, 'dp', across)]
    pallas_call x3, Pallas kernels: 182 us -> 174 us  [the longest x1 172 us: sums(): pl.pallas_call(kernel, out_shape=(pltpu.VMEM((n, d, ff), jnp.bfloat16), p...]
    ppermute x3 -> x5, waiting for transfers between devices: 7.1 us -> 2.3 us  [the longest x1 1.77 us: sums(): late0 = lax.ppermute(mine[1], 'dp', cross)]
  transfers between devices with their start and end apart: 3 -> 5, of which waited for: 1 -> 2; matrix products, arithmetic and copies ran while one was open for 0% -> 0% of each run, Pallas kernels for 3% -> 4%
where the time goes in v6:
time: 193 us
  Pallas kernels  180 us (93%)
  starting transfers between devices  10.9 us (6%)
  waiting for transfers between devices  2.3 us (1%)
    pallas_call x1, Pallas kernels, sums(): pl.pallas_call(kernel, out_shape=(pltpu.VMEM((n, d, ff), jnp.bfloat16), p...  172 us
    pallas_call x1, Pallas kernels, sums(): pl.pallas_call(copy_out, out_shape=result, in_specs=[vmem], out_specs=hbm...  5.9 us
    ppermute x1, starting transfers between devices, sums(): late0_other = lax.ppermute(late0, 'dp', across)  4.39 us
  transfers between devices with their start and end apart: 5, of which 2 were waited for; matrix products, arithmetic and copies ran while one was open for 0% of the time, Pallas kernels for 4%

profile of v6, /device:TPU:0, one launch (start us, length us, event | category | flops | bytes accessed | tf_op | source)
XLA Modules:
  0.0 193.1 jit_solution(15232330710270734530)
XLA Ops:
  0.0 171.9 %sums.1 = (bf16[4,896,2304]{2,1,0:T(8,128)(2,1)S(1)}, bf16[2,448,256]{2,1,0:T(8,128)(2,1)S(1)}, bf16[448,256]{1,0:T(8,128)(2,1)S(1)}, bf16[448,256]{1,0:T(8,128)...) custom-call(bf16[1,4,4096,896]{3,2,1,0:T(8,128)(2,1)} %a_ref.1, ...), custom_call_target="tpu_custom_call" | custom-call | tf_op jit(solution)/shard_map/sums/pallas_call | solution.py:375
  172.0 0.0 collective-permute-start.1
  172.0 2.0 %collective-permute-start.3 = (bf16[448,256]{1,0:T(8,128)(2,1)S(1)}, bf16[448,256]{1,0:T(8,128)(2,1)S(1)}, u32[]{:S(2)}, u32[]{:S(2)}) collective-permute-start(bf16[448,256]{1,0:T(8,128)(2,1)S(1)} %get-tuple-element.19.mine), channel_id=1, source_target_pairs={{0,2},{2,0},{1,3},{3,1},{4,6},{6,4},{5,7},{7,5}} | collective-permute-start | bytes 688136 | tf_op jit(solution)/shard_map/ppermute | solution.py:411
  174.0 2.5 %collective-permute-start = (bf16[2,448,256]{2,1,0:T(8,128)(2,1)S(1)}, bf16[2,448,256]{2,1,0:T(8,128)(2,1)S(1)}, u32[]{:S(2)}, u32[]{:S(2)}) collective-permute-start(bf16[2,448,256]{2,1,0:T(8,128)(2,1)S(1)} %get-tuple-element.18.got), channel_id=1, source_target_pairs={{0,1},{1,0},{2,3},{3,2},{4,5},{5,4},{6,7},{7,6}} | collective-permute-start | bytes 1376264 | tf_op jit(solution)/shard_map/ppermute | solution.py:422
  176.5 1.8 collective-permute-done.1.late
  178.3 4.4 %collective-permute-start.2 = (bf16[448,256]{1,0:T(8,128)(2,1)S(1)}, bf16[448,256]{1,0:T(8,128)(2,1)S(1)}, u32[]{:S(2)}, u32[]{:S(2)}) collective-permute-start(bf16[448,256]{1,0:T(8,128)(2,1)S(1)} %collective-permute-done.1.late), channel_id=1, source_target_pairs={{0,1},{1,0},{2,3},{3,2},{4,5},{5,4},{6,7},{7,6}} | collective-permute-start | bytes 688136 | tf_op jit(solution)/shard_map/ppermute | solution.py:423
  182.7 0.5 collective-permute-done.3.got
  183.2 2.0 %collective-permute-start.4 = (bf16[448,256]{1,0:T(8,128)(2,1)S(1)}, bf16[448,256]{1,0:T(8,128)(2,1)S(1)}, u32[]{:S(2)}, u32[]{:S(2)}) collective-permute-start(bf16[448,256]{1,0:T(8,128)(2,1)S(1)} %collective-permute-done.3.got), channel_id=1, source_target_pairs={{0,1},{1,0},{2,3},{3,2},{4,5},{5,4},{6,7},{7,6}} | collective-permute-start | bytes 688136 | tf_op jit(solution)/shard_map/ppermute | solution.py:424
  185.2 5.9 %copy_out.1.so_far = bf16[4,896,2304]{2,1,0:T(8,128)(2,1)} custom-call(bf16[4,896,2304]{2,1,0:T(8,128)(2,1)S(1)} %get-tuple-element.13.x_ref), custom_call_target="tpu_custom_call" | custom-call | flops 10000000000 | bytes 16515072 | tf_op jit(solution)/shard_map/copy_out/pallas_call | solution.py:412
  191.1 0.0 collective-permute-done.2.late_other
  191.1 0.0 collective-permute-done.got_other
  191.1 1.2 add.2.so_far
  192.3 0.0 collective-permute-done.4.got_other
  192.3 0.8 add.3
Async XLA Ops:
  172.0 6.4 %collective-permute-start.1 = (bf16[448,256]{1,0:T(8,128)(2,1)S(1)}, bf16[448,256]{1,0:T(8,128)(2,1)S(1)}, u32[]{:S(2)}, u32[]{:S(2)}) collective-permute-start(bf16[448,256]{1,0:T(8,128)(2,1)S(1)} %get-tuple-element.16.mine1), channel_id=1, source_target_pairs={{0,2},{2,0},{1,3},{3,1},{4,6},{6,4},{5,7},{7,5}} | collective-permute-start | bytes 688136 | tf_op jit(solution)/shard_map/ppermute | solution.py:410
  172.0 11.2 %collective-permute-start.3 = (bf16[448,256]{1,0:T(8,128)(2,1)S(1)}, bf16[448,256]{1,0:T(8,128)(2,1)S(1)}, u32[]{:S(2)}, u32[]{:S(2)}) collective-permute-start(bf16[448,256]{1,0:T(8,128)(2,1)S(1)} %get-tuple-element.19.mine), channel_id=1, source_target_pairs={{0,2},{2,0},{1,3},{3,1},{4,6},{6,4},{5,7},{7,5}} | collective-permute-start | bytes 688136 | tf_op jit(solution)/shard_map/ppermute | solution.py:411
  174.0 17.1 %collective-permute-start = (bf16[2,448,256]{2,1,0:T(8,128)(2,1)S(1)}, bf16[2,448,256]{2,1,0:T(8,128)(2,1)S(1)}, u32[]{:S(2)}, u32[]{:S(2)}) collective-permute-start(bf16[2,448,256]{2,1,0:T(8,128)(2,1)S(1)} %get-tuple-element.18.got), channel_id=1, source_target_pairs={{0,1},{1,0},{2,3},{3,2},{4,5},{5,4},{6,7},{7,6}} | collective-permute-start | bytes 1376264 | tf_op jit(solution)/shard_map/ppermute | solution.py:422
  178.3 12.8 %collective-permute-start.2 = (bf16[448,256]{1,0:T(8,128)(2,1)S(1)}, bf16[448,256]{1,0:T(8,128)(2,1)S(1)}, u32[]{:S(2)}, u32[]{:S(2)}) collective-permute-start(bf16[448,256]{1,0:T(8,128)(2,1)S(1)} %collective-permute-done.1.late), channel_id=1, source_target_pairs={{0,1},{1,0},{2,3},{3,2},{4,5},{5,4},{6,7},{7,6}} | collective-permute-start | bytes 688136 | tf_op jit(solution)/shard_map/ppermute | solution.py:423
  183.2 9.1 %collective-permute-start.4 = (bf16[448,256]{1,0:T(8,128)(2,1)S(1)}, bf16[448,256]{1,0:T(8,128)(2,1)S(1)}, u32[]{:S(2)}, u32[]{:S(2)}) collective-permute-start(bf16[448,256]{1,0:T(8,128)(2,1)S(1)} %collective-permute-done.3.got), channel_id=1, source_target_pairs={{0,1},{1,0},{2,3},{3,2},{4,5},{5,4},{6,7},{7,6}} | collective-permute-start | bytes 688136 | tf_op jit(solution)/shard_map/ppermute | solution.py:424
